TPU v7x, 32 devices: a whole 2x2x4 slice. The times are simulated.
32 devices in a mesh: rows: 8 (over z, x), cols: 4 (over y, core).
Axes of the slice: x: 2, y: 2, z: 4, core: 2. Of those that a mesh axis runs over, the one named last changes fastest.
Arguments:
- source: float32 [1024, 32768], P('rows', 'cols'), may hold values from -6 to 6
- low_row: int32 [1024], replicated, may hold values from 0 to 1022, as said below
- weight_low: float32 [1024], replicated, may hold values from 0 to 1
Outputs:
- mercator: float32 [1024, 32768], P('rows', 'cols')
- level1: float32 [512, 16384], P('rows', 'cols')
- level2: float32 [256, 8192], P('rows', 'cols')
- level3: float32 [128, 4096], P(('rows', 'cols'))
- level4: float32 [64, 2048], P(('rows', 'cols'))
Inputs may be any that keep to these rules, and one draw needn't show every extreme that they name: With t = 68 degrees in radians, E = ln tan(pi/4 + t/2), y = E * (1 - (2m + 1) / 2048) and lat = 2 atan(exp(y)) - pi/2, the base row of Mercator row m is floor((t - lat) / t * 1024 - 0.5) clipped to the range; low_row[m] differs from it by at most 2 and is then clipped to the range.
All inputs are finite; a program needn't handle non-finite values.
Results may differ from a plain program's by a relative error of at most 0.00007.
Values sent between devices are 32-bit elements; how exact they have to be, the bound alone decides.
A program may use at most 128 MiB of HBM per device.

v0:
```python
import math

import jax
import jax.numpy as jnp
from jax import lax
from jax.sharding import PartitionSpec as P


def blend(columns, low_row, weight_low):
    count = low_row.shape[0]
    both_rows = jnp.concatenate([low_row, low_row + 1], axis=0)
    fetched = jnp.take(columns, both_rows, axis=0)
    paired = fetched.reshape((2, count) + columns.shape[1:])
    scales = weight_low.reshape((-1,) + (1,) * (columns.ndim - 1))
    return scales * paired[0] + (1.0 - scales) * paired[1]


def halve(picture):
    height = picture.shape[0]
    width = picture.shape[1]
    stacked = picture.reshape(height // 2, 2, width)
    row_sums = stacked[:, 0, :] + stacked[:, 1, :]
    block = math.gcd(width, 256)
    inputs = lax.broadcasted_iota(jnp.int32, (block, block // 2), 0)
    outputs = lax.broadcasted_iota(jnp.int32, (block, block // 2), 1)
    pairing = jnp.where(inputs // 2 == outputs, 0.25, 0.0).astype(jnp.float32)
    blocks = row_sums.reshape(height // 2, width // block, block)
    pooled = jnp.einsum(
        "rkb,bo->rko",
        blocks,
        pairing,
        precision=lax.Precision.HIGHEST,
        preferred_element_type=jnp.float32,
    )
    return pooled.reshape(height // 2, width // 2)


def body(source, low_row, weight_low):
    columns = lax.all_to_all(source, "rows", split_axis=1, concat_axis=0, tiled=True)
    blended = blend(columns, low_row, weight_low)
    mercator = lax.all_to_all(blended, "rows", split_axis=0, concat_axis=1, tiled=True)
    level1 = halve(mercator)
    level2 = halve(level1)
    level3 = halve(level2)
    level3_rows = lax.all_to_all(level3, "cols", split_axis=0, concat_axis=1, tiled=True)
    level4_rows = halve(level3_rows)
    return (mercator, level1, level2, level3_rows, level4_rows)


def solution(mesh):
    placed = (P("rows", "cols"), P(), P())
    return jax.shard_map(
        body,
        mesh=mesh,
        in_specs=placed,
        out_specs=(
            P("rows", "cols"),
            P("rows", "cols"),
            P("rows", "cols"),
            P(("rows", "cols"), None),
            P(("rows", "cols"), None),
        ),
        check_vma=False,
    )
```

profile of v0, /device:TPU:0, one launch (start us, length us, event | category | flops | bytes accessed | tf_op | source)
XLA Modules:
  0.0 273.6 jit_solution(1395093125909395085)
XLA Ops:
  0.6 4.8 %copy.46 = f32[16,8,8,1024]{3,2,0,1:T(8,128)} copy(f32[16,8,8,1024]{3,2,1,0:T(8,128)} %bitcast.64) | data formatting | bytes 8388608 | tf_op jit(solution)/shard_map/all_to_all | solution.py:39
  5.4 0.0 copy-start
  5.4 0.0 copy-start.1
  5.4 7.4 %all-to-all-start = ((f32[128,8,1024]{2,0,1:T(8,128)}), f32[128,8,1024]{2,0,1:T(8,128)}, u32[]{:S(2)}, u32[]{:S(2)}) async-start(f32[128,8,1024]{2,0,1:T(8,128)} %bitcast.57), calls=%async_computation | async-start | bytes 8388608 | tf_op jit(solution)/shard_map/all_to_all | solution.py:39
  12.8 0.0 copy-done
  12.9 0.0 copy-done.1
  12.9 93.2 %all-to-all-done = f32[128,8,1024]{2,0,1:T(8,128)} async-done(((f32[128,8,1024]{2,0,1:T(8,128)}), f32[128,8,1024]{2,0,1:T(8,128)}, u32[]{:S(2)}, u32[]{:S(2)}) %all-to-all-start) | async-done | bytes 4194336 | tf_op jit(solution)/shard_map/all_to_all | solution.py:39
  106.1 13.9 %gather_fusion = f32[2048,1024]{1,0:T(8,128)} fusion(f32[1024,1024]{1,0:T(8,128)} %bitcast.2, s32[2048]{0:T(1024)S(1)} %broadcast_clamp_fusion), kind=kCustom, calls=%fused_computation | custom fusion | bytes 16785408 | tf_op jit(solution)/shard_map/jit(_take)/gather | solution.py:12
  120.1 3.8 %broadcast_select_fusion = f32[2048,1024]{1,0:T(8,128)S(1)} fusion(f32[2048,1024]{1,0:T(8,128)} %gather_fusion, pred[2048]{0:T(1024)(128)(4,1)S(1)} %compare_and_fusion), kind=kLoop, calls=%fused_computation.3 | loop fusion | flops 2097152 | bytes 16779264 | tf_op jit(solution)/shard_map/jit(_take)/select_n | solution.py:12
  123.9 1.7 fusion.45
  125.6 2.6 multiply_add_fusion
  128.2 4.5 %all-to-all-start.1 = ((f32[8,128,1024]{2,1,0:T(8,128)}), f32[8,128,1024]{2,1,0:T(8,128)}, u32[]{:S(2)}, u32[]{:S(2)}) async-start(f32[8,128,1024]{2,1,0:T(8,128)} %multiply_add_fusion), calls=%async_computation.1 | async-start | bytes 8388608 | tf_op jit(solution)/shard_map/all_to_all | solution.py:41
  132.7 92.5 %all-to-all-done.1 = f32[8,128,1024]{2,1,0:T(8,128)} async-done(((f32[8,128,1024]{2,1,0:T(8,128)}), f32[8,128,1024]{2,1,0:T(8,128)}, u32[]{:S(2)}, u32[]{:S(2)}) %all-to-all-start.1) | async-done | bytes 4194336 | tf_op jit(solution)/shard_map/all_to_all | solution.py:41
  225.3 6.6 %copy.26 = f32[128,8,1024]{2,1,0:T(8,128)} copy(f32[128,8,1024]{2,0,1:T(8,128)} %bitcast.11) | data formatting | bytes 8388608 | tf_op jit(solution)/shard_map/all_to_all | solution.py:41
  231.9 6.6 %reshape.168 = f32[64,2,8192]{2,1,0:T(2,128)} reshape(f32[128,8,1024]{2,1,0:T(8,128)} %copy.26) | data formatting | bytes 8388608 | tf_op jit(solution)/shard_map/reshape | solution.py:21
  238.5 9.4 %fusion = f32[64,8192]{1,0:T(8,128)S(1)} fusion(f32[64,2,8192]{2,1,0:T(2,128)} %reshape.168), kind=kLoop, calls=%fused_computation.5 | loop fusion | flops 524288 | bytes 6291456 | tf_op jit(solution)/shard_map/add | solution.py:22
  247.9 0.6 copy.31
  248.6 1.9 fusion.8
  250.5 0.6 reshape_reshape.6
  251.1 1.6 fusion.1
  252.7 0.2 copy.33
  252.8 0.7 fusion.6
  253.5 0.1 reshape_reshape.7
  253.7 0.4 fusion.2
  254.1 0.4 fusion.4
  254.6 0.7 all_to_all.47
  255.2 3.3 %all-to-all-start.2 = ((f32[4,4,1024]{2,1,0:T(4,128)}), f32[4,4,1024]{2,1,0:T(4,128)S(1)}, u32[]{:S(2)}, u32[]{:S(2)}) async-start(f32[4,4,1024]{2,1,0:T(4,128)} %all_to_all.47), calls=%async_computation.2 | async-start | bytes 131072 | tf_op jit(solution)/shard_map/all_to_all | solution.py:45
  258.5 0.8 copy.48
  259.3 1.6 copy.47
  260.9 5.3 %copy.25 = f32[8,128,1024]{1,2,0:T(8,128)} copy(f32[8,128,1024]{2,1,0:T(8,128)} %all-to-all-done.1) | data formatting | bytes 8388608 | tf_op jit(solution)/shard_map/all_to_all | solution.py:41
  266.2 5.6 %copy.28 = f32[128,8192]{1,0:T(8,128)} copy(f32[128,8192]{0,1:T(8,128)} %bitcast.58) | data formatting | bytes 8388608
  271.8 0.0 all-to-all-done.2
  271.8 0.1 reshape.171
  271.9 0.1 fusion.36
  272.0 0.3 convolution_bitcast_fusion
  272.4 0.6 copy.49
  273.0 0.6 copy.51
  (9 shorter events, 0.1 us)
Async XLA Ops:
  5.4 7.4 %copy-start = (s32[1024]{0:T(1024)S(1)}, s32[1024]{0:T(1024)}, u32[]{:S(2)}) copy-start(s32[1024]{0:T(1024)} %param.4) | copy-start | bytes 12292
  5.4 7.5 %copy-start.1 = (f32[1024]{0:T(1024)S(1)}, f32[1024]{0:T(1024)}, u32[]{:S(2)}) copy-start(f32[1024]{0:T(1024)} %param.5) | copy-start | bytes 12292
  5.4 100.7 %all-to-all-start = ((f32[128,8,1024]{2,0,1:T(8,128)}), f32[128,8,1024]{2,0,1:T(8,128)}, u32[]{:S(2)}, u32[]{:S(2)}) async-start(f32[128,8,1024]{2,0,1:T(8,128)} %bitcast.57), calls=%async_computation | async-start | bytes 8388608 | tf_op jit(solution)/shard_map/all_to_all | solution.py:39
  128.2 97.1 %all-to-all-start.1 = ((f32[8,128,1024]{2,1,0:T(8,128)}), f32[8,128,1024]{2,1,0:T(8,128)}, u32[]{:S(2)}, u32[]{:S(2)}) async-start(f32[8,128,1024]{2,1,0:T(8,128)} %multiply_add_fusion), calls=%async_computation.1 | async-start | bytes 8388608 | tf_op jit(solution)/shard_map/all_to_all | solution.py:41
  255.2 16.6 %all-to-all-start.2 = ((f32[4,4,1024]{2,1,0:T(4,128)}), f32[4,4,1024]{2,1,0:T(4,128)S(1)}, u32[]{:S(2)}, u32[]{:S(2)}) async-start(f32[4,4,1024]{2,1,0:T(4,128)} %all_to_all.47), calls=%async_computation.2 | async-start | bytes 131072 | tf_op jit(solution)/shard_map/all_to_all | solution.py:45
where the time goes:
time: 274 us
  waiting for transfers between devices  186 us (68%)
  local copies, waits for them, and re-layouts  50.4 us (18%)
  other arithmetic  18 us (7%)
  starting transfers between devices  15.2 us (6%)
  matrix products  3.4 us (1%)
    all_to_all x1, waiting for transfers between devices, body(): lax.all_to_all(source, 'rows', split_axis=1, concat_axis=0, tiled=True)  93.2 us
    all_to_all x1, waiting for transfers between devices, body(): lax.all_to_all(blended, 'rows', split_axis=0, concat_axis=1, tiled=True)  92.5 us
    gather x1, local copies, waits for them, and re-layouts, blend(): fetched = jnp.take(columns, both_rows, axis=0)  13.9 us
    all_to_all x2, local copies, waits for them, and re-layouts, body(): lax.all_to_all(blended, 'rows', split_axis=0, concat_axis=1, tiled=True)  11.9 us
    add x4, other arithmetic, halve(): row_sums = stacked[:, 0, :] + stacked[:, 1, :]  11.5 us
    unnamed x12, local copies, waits for them, and re-layouts  10 us
    all_to_all x1, starting transfers between devices, body(): lax.all_to_all(source, 'rows', split_axis=1, concat_axis=0, tiled=True)  7.41 us
    reshape x2, local copies, waits for them, and re-layouts, halve(): stacked = picture.reshape(height // 2, 2, width)  6.64 us
  transfers between devices with their start and end apart: 3, of which 2 were waited for; matrix products, arithmetic and copies ran while one was open for 5% of the time, Pallas kernels for 0%

commit v1 on v0

v1 whole, which is shorter than its diff:
```python
import functools
import math

import jax
import jax.numpy as jnp
import numpy as np
from jax import lax
from jax.experimental import pallas as pl
from jax.experimental.pallas import tpu as pltpu
from jax.sharding import PartitionSpec as P

CHUNK = 8
JITTER = 2
MESH = pl.DeviceIdType.MESH


def windows(total, parts):
    top = 68.0 * math.pi / 180.0
    edge = math.log(math.tan(math.pi / 4 + top / 2))
    m = np.arange(total, dtype=np.float64)
    y = edge * (1.0 - (2.0 * m + 1.0) / (2.0 * total))
    lat = 2.0 * np.arctan(np.exp(y)) - math.pi / 2
    pos = (top - lat) / top * total - 0.5
    slack = 0.01 * total / 1024
    first = np.clip(np.floor(pos - slack) - JITTER, 0, total - 2).astype(int)
    last = np.clip(np.floor(pos + slack) + JITTER, 0, total - 2).astype(int) + 1
    block = total // parts
    out = []
    for r in range(parts):
        low = int(first[r * block : (r + 1) * block].min())
        high = int(last[r * block : (r + 1) * block].max()) + 1
        low = low // CHUNK * CHUNK
        high = -(-high // CHUNK) * CHUNK
        assert high <= (r + 1) * block
        out.append((low, high))
    return out


def flows(total, parts):
    block = total // parts
    found = {}
    for d, (low, high) in enumerate(windows(total, parts)):
        for s in range(low // block, d):
            a, b = max(low, s * block), min(high, (s + 1) * block)
            if b > a:
                found[s, d] = ((a - s * block) // CHUNK, (b - a) // CHUNK)
    return found


def table(index, values):
    out = jnp.int32(values[0])
    for i in range(1, len(values)):
        if values[i] != values[i - 1]:
            out = jnp.where(index >= i, jnp.int32(values[i]), out)
    return out


def exchange_kernel(total, parts, source_ref, recv_ref, send_sem, recv_sem):
    me = lax.axis_index("rows")
    moves = flows(total, parts)
    wins = windows(total, parts)
    block = total // parts
    barrier = pltpu.get_barrier_semaphore()

    @pl.loop(1, parts)
    def _(i):
        pl.semaphore_signal(
            barrier, inc=1, device_id={"rows": lax.rem(me + i, parts)}, device_id_type=MESH
        )

    pl.semaphore_wait(barrier, parts - 1)

    def copy(chunk, slot, at, target):
        return pltpu.make_async_remote_copy(
            src_ref=source_ref.at[pl.ds(pl.multiple_of(chunk * CHUNK, CHUNK), CHUNK)],
            dst_ref=recv_ref.at[pl.ds(pl.multiple_of(slot * CHUNK, CHUNK), CHUNK)],
            send_sem=send_sem.at[at],
            recv_sem=recv_sem.at[slot],
            device_id={"rows": target},
            device_id_type=MESH,
        )

    deltas = sorted({d - s for s, d in moves})
    base = jnp.int32(0)
    for delta in deltas:
        first = table(me, [moves.get((s, s + delta), (0, 0))[0] for s in range(parts)])
        count = table(me, [moves.get((s, s + delta), (0, 0))[1] for s in range(parts)])
        slot0 = table(
            me,
            [
                s * (block // CHUNK) + moves[s, s + delta][0] - wins[s + delta][0] // CHUNK
                if (s, s + delta) in moves
                else 0
                for s in range(parts)
            ],
        )
        start = base
        target = lax.rem(me + delta, parts)

        @pl.loop(0, count)
        def _(i):
            copy(first + i, slot0 + i, start + i, target).start()

        base = base + count

    @pl.loop(0, base)
    def _(i):
        copy(0, 0, i, lax.rem(me + 1, parts)).wait_send()

    got = table(me, received(total, parts))

    @pl.loop(0, got)
    def _(i):
        copy(0, i, 0, lax.rem(me + 1, parts)).wait_recv()


def received(total, parts):
    moves = flows(total, parts)
    return [sum(n for (s, d), (_, n) in moves.items() if d == r) for r in range(parts)]


def exchange(source, total, parts):
    moves = flows(total, parts)
    slots = max(max(received(total, parts)), 2)
    slots += slots % 2
    sends = max(sum(n for (s, d), (_, n) in moves.items() if s == r) for r in range(parts))
    return pl.pallas_call(
        functools.partial(exchange_kernel, total, parts),
        out_shape=jax.ShapeDtypeStruct((slots * CHUNK, source.shape[1]), source.dtype),
        in_specs=[pl.BlockSpec(memory_space=pltpu.HBM)],
        out_specs=pl.BlockSpec(memory_space=pltpu.HBM),
        scratch_shapes=[
            pltpu.SemaphoreType.DMA((max(sends, 1),)),
            pltpu.SemaphoreType.DMA((slots,)),
        ],
        compiler_params=pltpu.CompilerParams(collective_id=0, has_side_effects=True),
        name="halo",
    )(source)


def split(x):
    high = x.astype(jnp.bfloat16)
    low = (x - high.astype(jnp.float32)).astype(jnp.bfloat16)
    return high, low


def pool_columns(x, levels):
    rows, width = x.shape
    slab = 128 << levels
    i = lax.broadcasted_iota(jnp.int32, (slab, 128), 0)
    o = lax.broadcasted_iota(jnp.int32, (slab, 128), 1)
    pairing = jnp.where(i >> levels == o, 0.5**levels, 0.0).astype(jnp.bfloat16)
    pieces = width // slab
    stacked = jnp.concatenate([x[:, k * slab : (k + 1) * slab] for k in range(pieces)], axis=0)
    high, low = split(stacked)
    out = jnp.dot(high, pairing, preferred_element_type=jnp.float32)
    out = out + jnp.dot(low, pairing, preferred_element_type=jnp.float32)
    return jnp.concatenate([out[k * rows : (k + 1) * rows] for k in range(pieces)], axis=1)


def pyramid_kernel(
    block, counts, aux_ref, own_ref, recv_ref, merc_ref, one_ref, two_ref, three_ref, wide
):
    slots = recv_ref.shape[0]
    depth = block + slots
    got = table(lax.axis_index("rows"), counts) * CHUNK

    @pl.when(pl.program_id(0) == 0)
    def _():
        col = lax.broadcasted_iota(jnp.int32, (block, depth), 1).astype(jnp.float32)
        weight = aux_ref[:, 2:3]
        band = jnp.where(col == aux_ref[:, 0:1], weight, 0.0)
        band = band + jnp.where(col == aux_ref[:, 1:2], 1.0 - weight, 0.0)
        parts = [band]
        for level in (1, 2, 3):
            o = lax.broadcasted_iota(jnp.int32, (block >> level, block), 0)
            i = lax.broadcasted_iota(jnp.int32, (block >> level, block), 1)
            pool = jnp.where(i >> level == o, 0.5**level, 0.0).astype(jnp.float32)
            parts.append(
                jnp.dot(
                    pool,
                    band,
                    precision=lax.Precision.HIGHEST,
                    preferred_element_type=jnp.float32,
                )
            )
        high, low = split(jnp.concatenate(parts, axis=0))
        wide[0] = high
        wide[1] = low

    row = lax.broadcasted_iota(jnp.int32, recv_ref.shape, 0)
    x = jnp.concatenate([own_ref[...], jnp.where(row < got, recv_ref[...], 0.0)], axis=0)
    high, low = split(x)
    y = jnp.dot(wide[0], high, preferred_element_type=jnp.float32)
    y = y + jnp.dot(wide[0], low, preferred_element_type=jnp.float32)
    y = y + jnp.dot(wide[1], high, preferred_element_type=jnp.float32)
    merc_ref[...] = y[:block]
    at = block
    for level, ref in ((1, one_ref), (2, two_ref), (3, three_ref)):
        n = block >> level
        ref[...] = pool_columns(y[at : at + n], level)
        at += n


def pyramid(aux, source, recv, total, parts):
    block, width = source.shape
    step = math.gcd(width, 1024)
    slots = recv.shape[0]
    wide_rows = block + block // 2 + block // 4 + block // 8
    return pl.pallas_call(
        functools.partial(pyramid_kernel, block, received(total, parts)),
        grid=(width // step,),
        out_shape=[
            jax.ShapeDtypeStruct((block >> k, width >> k), jnp.float32) for k in range(4)
        ],
        in_specs=[
            pl.BlockSpec(aux.shape, lambda j: (0, 0)),
            pl.BlockSpec((block, step), lambda j: (0, j)),
            pl.BlockSpec((slots, step), lambda j: (0, j)),
        ],
        out_specs=[pl.BlockSpec((block >> k, step >> k), lambda j: (0, j)) for k in range(4)],
        scratch_shapes=[pltpu.VMEM((2, wide_rows, block + slots), jnp.bfloat16)],
        name="pyramid",
    )(aux, source, recv)


def halve(x):
    r, c = x.shape
    x = x.reshape(r // 2, 2, c).sum(axis=1)
    i = lax.broadcasted_iota(jnp.int32, (c, c // 2), 0)
    o = lax.broadcasted_iota(jnp.int32, (c, c // 2), 1)
    pairing = jnp.where(i // 2 == o, 0.25, 0.0).astype(jnp.float32)
    return jnp.dot(x, pairing, precision=lax.Precision.HIGHEST)


def body(parts, source, low_row, weight_low):
    total = low_row.shape[0]
    block = source.shape[0]
    me = lax.axis_index("rows")
    recv = exchange(source, total, parts)
    lows = jnp.asarray([w[0] for w in windows(total, parts)], jnp.int32)
    mine = lax.dynamic_slice(low_row, (me * block,), (block,))
    weight = lax.dynamic_slice(weight_low, (me * block,), (block,))

    def place(g):
        return jnp.where(g >= me * block, g - me * block, block + g - lows[me])

    aux = jnp.stack(
        [place(mine).astype(jnp.float32), place(mine + 1).astype(jnp.float32), weight], axis=1
    )
    mercator, level1, level2, level3 = pyramid(aux, source, recv, total, parts)
    level4 = halve(level3)
    level3 = lax.all_to_all(level3, "cols", split_axis=0, concat_axis=1, tiled=True)
    level4 = lax.all_to_all(level4, "cols", split_axis=0, concat_axis=1, tiled=True)
    return mercator, level1, level2, level3, level4


def solution(mesh):
    return jax.shard_map(
        functools.partial(body, mesh.shape["rows"]),
        mesh=mesh,
        in_specs=(P("rows", "cols"), P(), P()),
        out_specs=(
            P("rows", "cols"),
            P("rows", "cols"),
            P("rows", "cols"),
            P(("rows", "cols"), None),
            P(("rows", "cols"), None),
        ),
        check_vma=False,
    )
```

time: 274 us -> 132 us (0.48)
  the two profiles are of different devices: /device:TPU:0 before, /device:TPU:10 now
where the time goes in v1:
time: 132 us; the launch traced here: 131 us
  Pallas kernels  108 us (82%)
  waiting for transfers between devices  7.25 us (5%)
  starting transfers between devices  6.54 us (5%)
  local copies, waits for them, and re-layouts  4.93 us (4%)
  matrix products  2.2 us (2%)
  other arithmetic  1.51 us (1%)
    pallas_call x1, Pallas kernels, exchange(): pl.pallas_call(functools.partial(exchange_kernel, total, parts), out_shap...  95 us
    pallas_call x1, Pallas kernels, pyramid(): pl.pallas_call(functools.partial(pyramid_kernel, block, received(total, p...  12.9 us
    all_to_all x1, waiting for transfers between devices, body(): lax.all_to_all(level3, 'cols', split_axis=0, concat_axis=1, tiled=True)  4.09 us
    all_to_all x1, starting transfers between devices, body(): lax.all_to_all(level3, 'cols', split_axis=0, concat_axis=1, tiled=True)  3.29 us
    all_to_all x1, starting transfers between devices, body(): lax.all_to_all(level4, 'cols', split_axis=0, concat_axis=1, tiled=True)  3.25 us
    all_to_all x1, waiting for transfers between devices, body(): lax.all_to_all(level4, 'cols', split_axis=0, concat_axis=1, tiled=True)  3.16 us
  transfers between devices with their start and end apart: 2, of which 2 were waited for; matrix products, arithmetic and copies ran while one was open for 0% of the time, Pallas kernels for 0%

profile of v1, /device:TPU:10, one launch (start us, length us, event | category | flops | bytes accessed | tf_op | source)
XLA Modules:
  0.0 131.1 jit_solution(742492888856974197)
XLA Ops:
  0.6 0.0 copy-start
  0.7 1.2 dynamic_slice.11
  1.9 0.0 copy-done
  1.9 0.1 dynamic-slice_bitcast_fusion
  2.0 1.4 %fusion.12 = (f32[128,1]{0,1:T(1,128)S(1)}, f32[128,1]{0,1:T(1,128)S(1)}) fusion(s32[]{:T(128)} %bitcast, s32[]{:T(128)S(6)} %mul.2, s32[1024]{0:T(1024)} %param.5, s32[]{:T(128)S(6)} %select_n.24), kind=kLoop, calls=%fused_computation.20 | loop fusion | flops 1664 | bytes 1548 | tf_op jit(solution)/shard_map/stack | solution.py:248
  3.4 0.7 copy.18.aux_ref
  4.2 95.0 %halo.1.recv_ref = f32[144,8192]{1,0:T(8,128)} custom-call(f32[128,8192]{1,0:T(8,128)} %own_ref.1), custom_call_target="tpu_custom_call" | custom-call | tf_op jit(solution)/shard_map/halo/pallas_call | solution.py:127
  99.1 12.9 %pyramid.1 = (f32[128,8192]{1,0:T(8,128)}, f32[64,4096]{1,0:T(8,128)}, f32[32,2048]{1,0:T(8,128)}, f32[16,1024]{1,0:T(8,128)}) custom-call(f32[128,3]{1,0:T(8,128)} %copy.18.aux_ref, f32[128,8192]{1,0:T(8,128)} %own_ref.1, f32[144,8192]{1,0:T(8,128)} %halo.1.recv_ref), custom_call_target="tpu_custom_call" | custom-call | tf_op jit(solution)/shard_map/pyramid/pallas_call | solution.py:210
  112.1 0.0 copy-start.1
  112.1 0.9 reshape.20
  113.0 0.1 reduce_sum.9
  113.2 2.2 %fusion = f32[4,2,512]{2,1,0:T(2,128)} fusion(f32[4,2,1024]{2,1,0:T(2,128)S(1)} %dot_general.5, s32[1024]{0:T(1024)S(1)} %get-tuple-element.15, s32[1024]{0:T(1024)S(1)} %get-tuple-element.16, pred[1024]{0:T(1024)(128)(4,1)S(1)} %fusion.10), kind=kOutput, calls=%fused_computation | convolution fusion | flops 51904512 | bytes 58368 | tf_op jit(solution)/shard_map/dot_general | solution.py:233
  115.4 3.3 %all-to-all-start.1 = ((f32[4,2,512]{2,1,0:T(2,128)}), f32[4,2,512]{2,1,0:T(2,128)S(1)}, u32[]{:S(2)}, u32[]{:S(2)}) async-start(f32[4,2,512]{2,1,0:T(2,128)} %fusion), calls=%async_computation.1 | async-start | bytes 32768 | tf_op jit(solution)/shard_map/all_to_all | solution.py:254
  118.6 0.0 copy-done.1
  118.6 0.7 all_to_all.26
  119.3 3.2 %all-to-all-done.1 = f32[4,2,512]{2,1,0:T(2,128)S(1)} async-done(((f32[4,2,512]{2,1,0:T(2,128)}), f32[4,2,512]{2,1,0:T(2,128)S(1)}, u32[]{:S(2)}, u32[]{:S(2)}) %all-to-all-start.1) | async-done | bytes 16416 | tf_op jit(solution)/shard_map/all_to_all | solution.py:254
  122.4 3.3 %all-to-all-start = ((f32[4,4,1024]{2,1,0:T(4,128)}), f32[4,4,1024]{2,1,0:T(4,128)S(1)}, u32[]{:S(2)}, u32[]{:S(2)}) async-start(f32[4,4,1024]{2,1,0:T(4,128)} %all_to_all.26), calls=%async_computation | async-start | bytes 131072 | tf_op jit(solution)/shard_map/all_to_all | solution.py:253
  125.7 4.1 %all-to-all-done = f32[4,4,1024]{2,1,0:T(4,128)S(1)} async-done(((f32[4,4,1024]{2,1,0:T(4,128)}), f32[4,4,1024]{2,1,0:T(4,128)S(1)}, u32[]{:S(2)}, u32[]{:S(2)}) %all-to-all-start) | async-done | bytes 65568 | tf_op jit(solution)/shard_map/all_to_all | solution.py:253
  129.8 0.6 copy.26
  130.5 0.6 copy.27
  (4 shorter events, 0.0 us)
Async XLA Ops:
  0.6 1.3 copy-start
  112.1 6.5 %copy-start.1 = (f32[16,1024]{1,0:T(8,128)S(1)}, f32[16,1024]{1,0:T(8,128)}, u32[]{:S(2)}) copy-start(f32[16,1024]{1,0:T(8,128)} %get-tuple-element.12) | copy-start | bytes 196612
  115.4 7.1 %all-to-all-start.1 = ((f32[4,2,512]{2,1,0:T(2,128)}), f32[4,2,512]{2,1,0:T(2,128)S(1)}, u32[]{:S(2)}, u32[]{:S(2)}) async-start(f32[4,2,512]{2,1,0:T(2,128)} %fusion), calls=%async_computation.1 | async-start | bytes 32768 | tf_op jit(solution)/shard_map/all_to_all | solution.py:254
  122.4 7.4 %all-to-all-start = ((f32[4,4,1024]{2,1,0:T(4,128)}), f32[4,4,1024]{2,1,0:T(4,128)S(1)}, u32[]{:S(2)}, u32[]{:S(2)}) async-start(f32[4,4,1024]{2,1,0:T(4,128)} %all_to_all.26), calls=%async_computation | async-start | bytes 131072 | tf_op jit(solution)/shard_map/all_to_all | solution.py:253

commit v2 on v1

v2 whole, which is shorter than its diff:
```python
import functools
import math

import jax
import jax.numpy as jnp
import numpy as np
from jax import lax
from jax.experimental import pallas as pl
from jax.experimental.pallas import tpu as pltpu
from jax.sharding import PartitionSpec as P

CHUNK = 8
JITTER = 2
MESH = pl.DeviceIdType.MESH


def windows(total, parts):
    top = 68.0 * math.pi / 180.0
    edge = math.log(math.tan(math.pi / 4 + top / 2))
    m = np.arange(total, dtype=np.float64)
    y = edge * (1.0 - (2.0 * m + 1.0) / (2.0 * total))
    lat = 2.0 * np.arctan(np.exp(y)) - math.pi / 2
    pos = (top - lat) / top * total - 0.5
    slack = 0.01 * total / 1024
    first = np.clip(np.floor(pos - slack) - JITTER, 0, total - 2).astype(int)
    last = np.clip(np.floor(pos + slack) + JITTER, 0, total - 2).astype(int) + 1
    block = total // parts
    out = []
    for r in range(parts):
        low = int(first[r * block : (r + 1) * block].min())
        high = int(last[r * block : (r + 1) * block].max()) + 1
        low = low // CHUNK * CHUNK
        high = -(-high // CHUNK) * CHUNK
        assert high <= (r + 1) * block
        out.append((low, high))
    return out


def flows(total, parts):
    block = total // parts
    found = {}
    for d, (low, high) in enumerate(windows(total, parts)):
        for s in range(low // block, d):
            a, b = max(low, s * block), min(high, (s + 1) * block)
            if b > a:
                found[s, d] = ((a - s * block) // CHUNK, (b - a) // CHUNK)
    return found


def table(index, values):
    out = jnp.int32(values[0])
    for i in range(1, len(values)):
        if values[i] != values[i - 1]:
            out = jnp.where(index >= i, jnp.int32(values[i]), out)
    return out


def relays(total, parts):
    moves = flows(total, parts)
    if max((d - s for s, d in moves), default=0) > 2:
        return {}
    load = {(p, z): 0 for p in (0, 1) for z in range(parts // 2)}
    for (s, d), (_, n) in moves.items():
        if d == s + 1:
            load[s % 2, d // 2] += n
    plan = {}
    while True:
        best = None
        for (s, d), (_, n) in moves.items():
            if d != s + 1:
                continue
            here = d // 2
            for there in (here - 1, here + 1) if s % 2 == 0 else (here - 1,):
                if not 0 <= there < parts // 2:
                    continue
                relay = d + 2 * (there - here)
                used = plan.get((s, d), (relay, 0))
                taken = any(v[0] == relay and k != (s, d) for k, v in plan.items())
                if used[0] != relay or used[1] >= n or taken:
                    continue
                gap = load[s % 2, here] - load[s % 2, there]
                if gap >= 2 and (best is None or gap > best[0]):
                    best = (gap, s, d, here, there, relay, used[1] + 1)
        if best is None:
            return plan
        _, s, d, here, there, relay, n = best
        plan[s, d] = (relay, n)
        load[s % 2, here] -= 1
        load[s % 2, there] += 1


def exchange_kernel(total, parts, source_ref, recv_ref, held, send_sem, recv_sem, held_sem):
    me = lax.axis_index("rows")
    moves = flows(total, parts)
    wins = windows(total, parts)
    plan = relays(total, parts)
    block = total // parts
    barrier = pltpu.get_barrier_semaphore()

    @pl.loop(1, parts)
    def _(i):
        pl.semaphore_signal(
            barrier, inc=1, device_id={"rows": lax.rem(me + i, parts)}, device_id_type=MESH
        )

    pl.semaphore_wait(barrier, parts - 1)

    def chunk_of(ref, at):
        return ref.at[pl.ds(pl.multiple_of(at * CHUNK, CHUNK), CHUNK)]

    def copy(src, dst, at, landed, target):
        return pltpu.make_async_remote_copy(
            src_ref=src,
            dst_ref=dst,
            send_sem=send_sem.at[at],
            recv_sem=landed,
            device_id={"rows": target},
            device_id_type=MESH,
        )

    def slot_of(s, d):
        return s * (block // CHUNK) + moves[s, d][0] - wins[d][0] // CHUNK

    base = jnp.int32(0)
    by_source = {s: (r - s, moves[s, d][0], n) for (s, d), (r, n) in plan.items()}
    for shift in sorted({v[0] for v in by_source.values()}):
        mine = [by_source.get(s, (0, 0, 0)) for s in range(parts)]
        mine = [v if v[0] == shift else (0, 0, 0) for v in mine]
        first = table(me, [v[1] for v in mine])
        count = table(me, [v[2] for v in mine])
        start = base
        target = lax.rem(me + shift + parts, parts)

        @pl.loop(0, count)
        def _(i):
            copy(
                chunk_of(source_ref, first + i),
                chunk_of(held, i),
                start + i,
                held_sem.at[i],
                target,
            ).start()

        base = base + count

    for delta in sorted({d - s for s, d in moves}):
        ours = [(s, s + delta) for s in range(parts)]
        skip = [plan.get(k, (0, 0))[1] for k in ours]
        first = table(me, [moves[k][0] + n if k in moves else 0 for k, n in zip(ours, skip)])
        count = table(me, [moves[k][1] - n if k in moves else 0 for k, n in zip(ours, skip)])
        slot0 = table(me, [slot_of(*k) + n if k in moves else 0 for k, n in zip(ours, skip)])
        start = base
        target = lax.rem(me + delta, parts)

        @pl.loop(0, count)
        def _(i):
            copy(
                chunk_of(source_ref, first + i),
                chunk_of(recv_ref, slot0 + i),
                start + i,
                recv_sem.at[slot0 + i],
                target,
            ).start()

        base = base + count

    by_relay = {r: (d - r, slot_of(s, d), n) for (s, d), (r, n) in plan.items()}
    for shift in sorted({v[0] for v in by_relay.values()}):
        mine = [by_relay.get(r, (0, 0, 0)) for r in range(parts)]
        mine = [v if v[0] == shift else (0, 0, 0) for v in mine]
        slot0 = table(me, [v[1] for v in mine])
        count = table(me, [v[2] for v in mine])
        start = base
        target = lax.rem(me + shift + parts, parts)

        @pl.loop(0, count)
        def _(i):
            forward = copy(
                chunk_of(held, i),
                chunk_of(recv_ref, slot0 + i),
                start + i,
                recv_sem.at[slot0 + i],
                target,
            )
            copy(
                chunk_of(source_ref, 0), chunk_of(held, i), 0, held_sem.at[i], target
            ).wait_recv()
            forward.start()

        base = base + count

    other = lax.rem(me + 1, parts)

    @pl.loop(0, base)
    def _(i):
        copy(
            chunk_of(source_ref, 0), chunk_of(recv_ref, 0), i, recv_sem.at[0], other
        ).wait_send()

    got = table(me, received(total, parts))

    @pl.loop(0, got)
    def _(i):
        copy(
            chunk_of(source_ref, 0), chunk_of(recv_ref, i), 0, recv_sem.at[i], other
        ).wait_recv()


def received(total, parts):
    moves = flows(total, parts)
    return [sum(n for (s, d), (_, n) in moves.items() if d == r) for r in range(parts)]


def exchange(source, total, parts):
    moves = flows(total, parts)
    slots = max(max(received(total, parts)), 2)
    slots += slots % 2
    plan = relays(total, parts)
    sends = max(
        sum(n for (s, d), (_, n) in moves.items() if s == p)
        + sum(n for r, n in plan.values() if r == p)
        for p in range(parts)
    )
    hold = max([n for _, n in plan.values()], default=1)
    return pl.pallas_call(
        functools.partial(exchange_kernel, total, parts),
        out_shape=jax.ShapeDtypeStruct((slots * CHUNK, source.shape[1]), source.dtype),
        in_specs=[pl.BlockSpec(memory_space=pltpu.HBM)],
        out_specs=pl.BlockSpec(memory_space=pltpu.HBM),
        scratch_shapes=[
            pltpu.VMEM((hold * CHUNK, source.shape[1]), source.dtype),
            pltpu.SemaphoreType.DMA((max(sends, 1),)),
            pltpu.SemaphoreType.DMA((slots,)),
            pltpu.SemaphoreType.DMA((hold,)),
        ],
        compiler_params=pltpu.CompilerParams(collective_id=0, has_side_effects=True),
        name="halo",
    )(source)


def split(x):
    high = x.astype(jnp.bfloat16)
    low = (x - high.astype(jnp.float32)).astype(jnp.bfloat16)
    return high, low


def pool_columns(x, levels):
    rows, width = x.shape
    slab = 128 << levels
    i = lax.broadcasted_iota(jnp.int32, (slab, 128), 0)
    o = lax.broadcasted_iota(jnp.int32, (slab, 128), 1)
    pairing = jnp.where(i >> levels == o, 0.5**levels, 0.0).astype(jnp.bfloat16)
    pieces = width // slab
    stacked = jnp.concatenate([x[:, k * slab : (k + 1) * slab] for k in range(pieces)], axis=0)
    high, low = split(stacked)
    out = jnp.dot(high, pairing, preferred_element_type=jnp.float32)
    out = out + jnp.dot(low, pairing, preferred_element_type=jnp.float32)
    return jnp.concatenate([out[k * rows : (k + 1) * rows] for k in range(pieces)], axis=1)


def pyramid_kernel(
    total, parts, low_ref, weight_ref, own_ref, recv_ref, merc_ref, one_ref, two_ref, three_ref, wide
):
    block = own_ref.shape[0]
    slots = recv_ref.shape[0]
    depth = block + slots
    me = lax.axis_index("rows")
    got = table(me, received(total, parts)) * CHUNK

    @pl.when(pl.program_id(0) == 0)
    def _():
        begin = table(me, [w[0] for w in windows(total, parts)])
        low = low_ref[pl.ds(me, 1), :]
        weight = weight_ref[pl.ds(me, 1), :]

        def place(g):
            return jnp.where(g >= me * block, g - me * block, block + g - begin)

        k = lax.broadcasted_iota(jnp.int32, (depth, block), 0)
        band = jnp.where(k == place(low), weight, 0.0)
        band = band + jnp.where(k == place(low + 1), 1.0 - weight, 0.0)
        pools = []
        for level in range(4):
            o = lax.broadcasted_iota(jnp.int32, (block >> level, block), 0)
            i = lax.broadcasted_iota(jnp.int32, (block >> level, block), 1)
            pools.append(jnp.where(i >> level == o, 0.5**level, 0.0).astype(jnp.float32))
        rows = lax.dot_general(
            jnp.concatenate(pools, axis=0),
            band,
            (((1,), (1,)), ((), ())),
            precision=lax.Precision.HIGHEST,
            preferred_element_type=jnp.float32,
        )
        high, low_part = split(rows)
        wide[...] = jnp.concatenate([high, high, low_part], axis=1)

    row = lax.broadcasted_iota(jnp.int32, recv_ref.shape, 0)
    x = jnp.concatenate([own_ref[...], jnp.where(row < got, recv_ref[...], 0.0)], axis=0)
    high, low_part = split(x)
    stacked = jnp.concatenate([high, low_part, high], axis=0)
    y = jnp.dot(wide[...], stacked, preferred_element_type=jnp.float32)
    merc_ref[...] = y[:block]
    at = block
    for level, ref in ((1, one_ref), (2, two_ref)):
        n = block >> level
        ref[...] = pool_columns(y[at : at + n], level)
        at += n
    three = pool_columns(y[at:], 3)
    each = three_ref.shape[1]
    for i in range(three_ref.shape[0]):
        three_ref[i] = three[i * each : (i + 1) * each]


def pyramid(low_row, weight_low, source, recv, total, parts, owners):
    block, width = source.shape
    step = math.gcd(width, 1024)
    slots = recv.shape[0]
    wide_rows = block + block // 2 + block // 4 + block // 8
    each = (block >> 3) // owners
    return pl.pallas_call(
        functools.partial(pyramid_kernel, total, parts),
        grid=(width // step,),
        out_shape=[jax.ShapeDtypeStruct((block >> k, width >> k), jnp.float32) for k in range(3)]
        + [jax.ShapeDtypeStruct((owners, each, width >> 3), jnp.float32)],
        in_specs=[
            pl.BlockSpec((parts, block), lambda j: (0, 0)),
            pl.BlockSpec((parts, block), lambda j: (0, 0)),
            pl.BlockSpec((block, step), lambda j: (0, j)),
            pl.BlockSpec((slots, step), lambda j: (0, j)),
        ],
        out_specs=[pl.BlockSpec((block >> k, step >> k), lambda j: (0, j)) for k in range(3)]
        + [pl.BlockSpec((owners, each, step >> 3), lambda j: (0, 0, j))],
        scratch_shapes=[pltpu.VMEM((wide_rows, 3 * (block + slots)), jnp.bfloat16)],
        name="pyramid",
    )(low_row.reshape(parts, block), weight_low.reshape(parts, block), source, recv)


def share_kernel(owners, three_ref, rows_ref, pooled_ref, landed, send_sem, recv_sem):
    me = lax.axis_index("cols")
    width = three_ref.shape[2]
    barrier = pltpu.get_barrier_semaphore()
    for i in range(1, owners):
        pl.semaphore_signal(
            barrier, inc=1, device_id={"cols": lax.rem(me + i, owners)}, device_id_type=MESH
        )
    pl.semaphore_wait(barrier, owners - 1)
    copies = []
    for i in range(1, owners):
        target = lax.rem(me + i, owners)
        copies.append(
            pltpu.make_async_remote_copy(
                src_ref=three_ref.at[target],
                dst_ref=landed.at[owners - i],
                send_sem=send_sem.at[i],
                recv_sem=recv_sem.at[owners - i],
                device_id={"cols": target},
                device_id_type=MESH,
            )
        )
    for c in copies:
        c.start()
    levels = 1
    slab = 128 << levels
    i = lax.broadcasted_iota(jnp.int32, (slab, 128), 0)
    o = lax.broadcasted_iota(jnp.int32, (slab, 128), 1)
    pairing = jnp.where(i >> levels == o, 0.25, 0.0).astype(jnp.bfloat16)

    def place(piece, column):
        rows_ref[:, pl.ds(pl.multiple_of(column * width, 128), width)] = piece
        pairs = piece.shape[0] // 2
        sums = jnp.concatenate(
            [piece[2 * p : 2 * p + 1] + piece[2 * p + 1 : 2 * p + 2] for p in range(pairs)], axis=0
        )
        flat = jnp.concatenate(
            [sums[:, k * slab : (k + 1) * slab] for k in range(width // slab)], axis=0
        )
        high, low_part = split(flat)
        out = jnp.dot(high, pairing, preferred_element_type=jnp.float32)
        out = out + jnp.dot(low_part, pairing, preferred_element_type=jnp.float32)
        out = jnp.concatenate(
            [out[k * pairs : (k + 1) * pairs] for k in range(width // slab)], axis=1
        )
        half = width // 2
        pooled_ref[:, pl.ds(pl.multiple_of(column * half, 128), half)] = out

    place(three_ref[me], me)
    for i in range(1, owners):
        copies[owners - i - 1].wait_recv()
        place(landed[i], lax.rem(me + i, owners))
    for c in copies:
        c.wait_send()


def share(three):
    owners, each, width = three.shape
    return pl.pallas_call(
        functools.partial(share_kernel, owners),
        out_shape=[
            jax.ShapeDtypeStruct((each, owners * width), jnp.float32),
            jax.ShapeDtypeStruct((each // 2, owners * width // 2), jnp.float32),
        ],
        in_specs=[pl.BlockSpec(memory_space=pltpu.VMEM)],
        out_specs=[pl.BlockSpec(memory_space=pltpu.VMEM)] * 2,
        scratch_shapes=[
            pltpu.VMEM(three.shape, jnp.float32),
            pltpu.SemaphoreType.DMA((owners,)),
            pltpu.SemaphoreType.DMA((owners,)),
        ],
        compiler_params=pltpu.CompilerParams(collective_id=1, has_side_effects=True),
        name="share",
    )(three)


def body(parts, owners, source, low_row, weight_low):
    total = low_row.shape[0]
    recv = exchange(source, total, parts)
    mercator, level1, level2, three = pyramid(
        low_row, weight_low, source, recv, total, parts, owners
    )
    level3, level4 = share(three)
    return mercator, level1, level2, level3, level4


def solution(mesh):
    return jax.shard_map(
        functools.partial(body, mesh.shape["rows"], mesh.shape["cols"]),
        mesh=mesh,
        in_specs=(P("rows", "cols"), P(), P()),
        out_specs=(
            P("rows", "cols"),
            P("rows", "cols"),
            P("rows", "cols"),
            P(("rows", "cols"), None),
            P(("rows", "cols"), None),
        ),
        check_vma=False,
    )
```

time: 132 us -> 95.5 us (0.72)
  the two profiles are of different devices: /device:TPU:10 before, /device:TPU:0 now
where the time goes in v2:
time: 95.5 us; the launch traced here: 95 us
  Pallas kernels  91.6 us (96%)
  local copies, waits for them, and re-layouts  2.8 us (3%)
    pallas_call x1, Pallas kernels, exchange(): pl.pallas_call(functools.partial(exchange_kernel, total, parts), out_shap...  74.2 us
    pallas_call x1, Pallas kernels, pyramid(): pl.pallas_call(functools.partial(pyramid_kernel, total, parts), grid=(wid...  11.8 us
    pallas_call x1, Pallas kernels, share(): pl.pallas_call(functools.partial(share_kernel, owners), out_shape=[jax.Sh...  5.58 us
    unnamed x2, local copies, waits for them, and re-layouts  2.8 us

profile of v2, /device:TPU:0, one launch (start us, length us, event | category | flops | bytes accessed | tf_op | source)
XLA Modules:
  0.0 95.0 jit_solution(16769559869739278280)
XLA Ops:
  0.6 74.2 %halo.1.recv_ref = f32[144,8192]{1,0:T(8,128)} custom-call(f32[128,8192]{1,0:T(8,128)} %own_ref.1), custom_call_target="tpu_custom_call" | custom-call | tf_op jit(solution)/shard_map/halo/pallas_call | solution.py:225
  74.8 11.8 %pyramid.1 = (f32[128,8192]{1,0:T(8,128)}, f32[64,4096]{1,0:T(8,128)}, f32[32,2048]{1,0:T(8,128)}, f32[4,4,1024]{2,1,0:T(4,128)}) custom-call(s32[8,128]{1,0:T(8,128)} %bitcast.2, f32[8,128]{1,0:T(8,128)} %bitcast.3, f32[128,8192]{1,0:T(8,128)} %own_ref.1, f32[144,8192]{1,0:T(8,128)} %halo.1.recv_ref), custom_call_target="tpu_custom_call" | custom-call | tf_op jit(solution)/shard_map/pyramid/pallas_call | solution.py:320
  86.6 5.6 %share.1 = (f32[4,4096]{1,0:T(4,128)}, f32[2,2048]{1,0:T(2,128)}) custom-call(f32[4,4,1024]{2,1,0:T(4,128)} %get-tuple-element.14.three_ref), custom_call_target="tpu_custom_call" | custom-call | tf_op jit(solution)/shard_map/share/pallas_call | solution.py:396
  92.2 1.5 %copy.10 = f32[4,4096]{1,0:T(4,128)} copy(f32[4,4096]{1,0:T(4,128)} %get-tuple-element.25) | data formatting | bytes 131072
  93.7 1.3 %copy.11 = f32[2,2048]{1,0:T(2,128)} copy(f32[2,2048]{1,0:T(2,128)} %get-tuple-element.26) | data formatting | bytes 32768

commit v3 on v2

--- a/solution.py
+++ b/solution.py
@@ -10,6 +10,8 @@
 from jax.sharding import PartitionSpec as P
 
 CHUNK = 8
+SPLIT = 2
+STEP = 2048
 JITTER = 2
 MESH = pl.DeviceIdType.MESH
 
@@ -47,6 +49,10 @@
     return found
 
 
+def units(total, parts):
+    return {k: (a * SPLIT, n * SPLIT) for k, (a, n) in flows(total, parts).items()}
+
+
 def table(index, values):
     out = jnp.int32(values[0])
     for i in range(1, len(values)):
@@ -56,42 +62,33 @@
 
 
 def relays(total, parts):
-    moves = flows(total, parts)
-    if max((d - s for s, d in moves), default=0) > 2:
+    moves = units(total, parts)
+    pairs = parts // 2
+    if max((d - s for s, d in moves), default=0) > 2 or parts % 2:
         return {}
-    load = {(p, z): 0 for p in (0, 1) for z in range(parts // 2)}
-    for (s, d), (_, n) in moves.items():
-        if d == s + 1:
-            load[s % 2, d // 2] += n
-    plan = {}
-    while True:
-        best = None
-        for (s, d), (_, n) in moves.items():
-            if d != s + 1:
+    plan, taken, before = {}, set(), {}
+    for parity in (0, 1):
+        flow = [(2 * z - parity, 2 * z - parity + 1) for z in range(pairs)]
+        load = [moves.get(k, (0, 0))[1] for k in flow]
+        goal = [sum(load) // pairs + (z < sum(load) % pairs) for z in range(pairs)]
+        across = 0
+        for z in range(pairs - 1):
+            across += load[z] - goal[z]
+            key = flow[z] if across > 0 else flow[z + 1]
+            relay = key[1] + (2 if across > 0 else -2)
+            used = before.get(key, 0)
+            n = min(abs(across), moves.get(key, (0, 0))[1] - used)
+            if n <= 0 or relay in taken or relay == key[0] or (parity and across > 0):
                 continue
-            here = d // 2
-            for there in (here - 1, here + 1) if s % 2 == 0 else (here - 1,):
-                if not 0 <= there < parts // 2:
-                    continue
-                relay = d + 2 * (there - here)
-                used = plan.get((s, d), (relay, 0))
-                taken = any(v[0] == relay and k != (s, d) for k, v in plan.items())
-                if used[0] != relay or used[1] >= n or taken:
-                    continue
-                gap = load[s % 2, here] - load[s % 2, there]
-                if gap >= 2 and (best is None or gap > best[0]):
-                    best = (gap, s, d, here, there, relay, used[1] + 1)
-        if best is None:
-            return plan
-        _, s, d, here, there, relay, n = best
-        plan[s, d] = (relay, n)
-        load[s % 2, here] -= 1
-        load[s % 2, there] += 1
+            plan[key + (relay,)] = (used, n)
+            before[key] = used + n
+            taken.add(relay)
+    return plan
 
 
 def exchange_kernel(total, parts, source_ref, recv_ref, held, send_sem, recv_sem, held_sem):
     me = lax.axis_index("rows")
-    moves = flows(total, parts)
+    moves = units(total, parts)
     wins = windows(total, parts)
     plan = relays(total, parts)
     block = total // parts
@@ -105,8 +102,15 @@
 
     pl.semaphore_wait(barrier, parts - 1)
 
+    piece = source_ref.shape[1] // SPLIT
+
     def chunk_of(ref, at):
-        return ref.at[pl.ds(pl.multiple_of(at * CHUNK, CHUNK), CHUNK)]
+        rows = pl.ds(pl.multiple_of(lax.div(at, SPLIT) * CHUNK, CHUNK), CHUNK)
+        columns = pl.ds(pl.multiple_of(lax.rem(at, SPLIT) * piece, piece), piece)
+        return ref.at[rows, columns]
+
+    def held_at(i):
+        return held.at[pl.ds(pl.multiple_of(i * CHUNK, CHUNK), CHUNK)]
 
     def copy(src, dst, at, landed, target):
         return pltpu.make_async_remote_copy(
@@ -119,15 +123,14 @@
         )
 
     def slot_of(s, d):
-        return s * (block // CHUNK) + moves[s, d][0] - wins[d][0] // CHUNK
+        return (s * block - wins[d][0]) // CHUNK * SPLIT + moves[s, d][0]
 
     base = jnp.int32(0)
-    by_source = {s: (r - s, moves[s, d][0], n) for (s, d), (r, n) in plan.items()}
-    for shift in sorted({v[0] for v in by_source.values()}):
-        mine = [by_source.get(s, (0, 0, 0)) for s in range(parts)]
-        mine = [v if v[0] == shift else (0, 0, 0) for v in mine]
-        first = table(me, [v[1] for v in mine])
-        count = table(me, [v[2] for v in mine])
+    by_source = {(s, r - s): (moves[s, d][0] + a, n) for (s, d, r), (a, n) in plan.items()}
+    for shift in sorted({k[1] for k in by_source}):
+        mine = [by_source.get((s, shift), (0, 0)) for s in range(parts)]
+        first = table(me, [v[0] for v in mine])
+        count = table(me, [v[1] for v in mine])
         start = base
         target = lax.rem(me + shift + parts, parts)
 
@@ -135,7 +138,7 @@
         def _(i):
             copy(
                 chunk_of(source_ref, first + i),
-                chunk_of(held, i),
+                held_at(i),
                 start + i,
                 held_sem.at[i],
                 target,
@@ -145,7 +148,7 @@
 
     for delta in sorted({d - s for s, d in moves}):
         ours = [(s, s + delta) for s in range(parts)]
-        skip = [plan.get(k, (0, 0))[1] for k in ours]
+        skip = [sum(v[1] for p, v in plan.items() if p[:2] == k) for k in ours]
         first = table(me, [moves[k][0] + n if k in moves else 0 for k, n in zip(ours, skip)])
         count = table(me, [moves[k][1] - n if k in moves else 0 for k, n in zip(ours, skip)])
         slot0 = table(me, [slot_of(*k) + n if k in moves else 0 for k, n in zip(ours, skip)])
@@ -164,26 +167,25 @@
 
         base = base + count
 
-    by_relay = {r: (d - r, slot_of(s, d), n) for (s, d), (r, n) in plan.items()}
-    for shift in sorted({v[0] for v in by_relay.values()}):
-        mine = [by_relay.get(r, (0, 0, 0)) for r in range(parts)]
-        mine = [v if v[0] == shift else (0, 0, 0) for v in mine]
-        slot0 = table(me, [v[1] for v in mine])
-        count = table(me, [v[2] for v in mine])
+    by_relay = {(r, d - r): (slot_of(s, d) + a, n) for (s, d, r), (a, n) in plan.items()}
+    for shift in sorted({k[1] for k in by_relay}):
+        mine = [by_relay.get((r, shift), (0, 0)) for r in range(parts)]
+        slot0 = table(me, [v[0] for v in mine])
+        count = table(me, [v[1] for v in mine])
         start = base
         target = lax.rem(me + shift + parts, parts)
 
         @pl.loop(0, count)
         def _(i):
             forward = copy(
-                chunk_of(held, i),
+                held_at(i),
                 chunk_of(recv_ref, slot0 + i),
                 start + i,
                 recv_sem.at[slot0 + i],
                 target,
             )
             copy(
-                chunk_of(source_ref, 0), chunk_of(held, i), 0, held_sem.at[i], target
+                chunk_of(source_ref, jnp.int32(0)), held_at(i), 0, held_sem.at[i], target
             ).wait_recv()
             forward.start()
 
@@ -194,15 +196,15 @@
     @pl.loop(0, base)
     def _(i):
         copy(
-            chunk_of(source_ref, 0), chunk_of(recv_ref, 0), i, recv_sem.at[0], other
+            chunk_of(source_ref, jnp.int32(0)), chunk_of(recv_ref, jnp.int32(0)), i, recv_sem.at[0], other
         ).wait_send()
 
-    got = table(me, received(total, parts))
+    got = table(me, received(total, parts)) * SPLIT
 
     @pl.loop(0, got)
     def _(i):
         copy(
-            chunk_of(source_ref, 0), chunk_of(recv_ref, i), 0, recv_sem.at[i], other
+            chunk_of(source_ref, jnp.int32(0)), chunk_of(recv_ref, i), 0, recv_sem.at[i], other
         ).wait_recv()
 
 
@@ -212,13 +214,13 @@
 
 
 def exchange(source, total, parts):
-    moves = flows(total, parts)
+    moves = units(total, parts)
     slots = max(max(received(total, parts)), 2)
     slots += slots % 2
     plan = relays(total, parts)
     sends = max(
         sum(n for (s, d), (_, n) in moves.items() if s == p)
-        + sum(n for r, n in plan.values() if r == p)
+        + sum(n for (_, _, r), (_, n) in plan.items() if r == p)
         for p in range(parts)
     )
     hold = max([n for _, n in plan.values()], default=1)
@@ -228,9 +230,9 @@
         in_specs=[pl.BlockSpec(memory_space=pltpu.HBM)],
         out_specs=pl.BlockSpec(memory_space=pltpu.HBM),
         scratch_shapes=[
-            pltpu.VMEM((hold * CHUNK, source.shape[1]), source.dtype),
+            pltpu.VMEM((hold * CHUNK, source.shape[1] // SPLIT), source.dtype),
             pltpu.SemaphoreType.DMA((max(sends, 1),)),
-            pltpu.SemaphoreType.DMA((slots,)),
+            pltpu.SemaphoreType.DMA((slots * SPLIT,)),
             pltpu.SemaphoreType.DMA((hold,)),
         ],
         compiler_params=pltpu.CompilerParams(collective_id=0, has_side_effects=True),
@@ -313,7 +315,7 @@
 
 def pyramid(low_row, weight_low, source, recv, total, parts, owners):
     block, width = source.shape
-    step = math.gcd(width, 1024)
+    step = math.gcd(width, STEP)
     slots = recv.shape[0]
     wide_rows = block + block // 2 + block // 4 + block // 8
     each = (block >> 3) // owners
@@ -335,14 +337,15 @@
     )(low_row.reshape(parts, block), weight_low.reshape(parts, block), source, recv)
 
 
-def share_kernel(owners, three_ref, rows_ref, pooled_ref, landed, send_sem, recv_sem):
+def share_kernel(owners, three_ref, landed, send_sem, recv_sem, own_sem):
     me = lax.axis_index("cols")
-    width = three_ref.shape[2]
     barrier = pltpu.get_barrier_semaphore()
     for i in range(1, owners):
         pl.semaphore_signal(
             barrier, inc=1, device_id={"cols": lax.rem(me + i, owners)}, device_id_type=MESH
         )
+    own = pltpu.make_async_copy(three_ref.at[me], landed.at[0], own_sem)
+    own.start()
     pl.semaphore_wait(barrier, owners - 1)
     copies = []
     for i in range(1, owners):
@@ -359,56 +362,60 @@
         )
     for c in copies:
         c.start()
-    levels = 1
-    slab = 128 << levels
+    own.wait()
+    for c in copies:
+        c.wait()
+
+
+def finish_kernel(landed, rows_ref, pooled_ref):
+    owners, each, width = landed.shape
+    me = lax.axis_index("cols")
+    pairs = each // 2
+    slab = 256
     i = lax.broadcasted_iota(jnp.int32, (slab, 128), 0)
     o = lax.broadcasted_iota(jnp.int32, (slab, 128), 1)
-    pairing = jnp.where(i >> levels == o, 0.25, 0.0).astype(jnp.bfloat16)
-
-    def place(piece, column):
-        rows_ref[:, pl.ds(pl.multiple_of(column * width, 128), width)] = piece
-        pairs = piece.shape[0] // 2
-        sums = jnp.concatenate(
-            [piece[2 * p : 2 * p + 1] + piece[2 * p + 1 : 2 * p + 2] for p in range(pairs)], axis=0
-        )
-        flat = jnp.concatenate(
-            [sums[:, k * slab : (k + 1) * slab] for k in range(width // slab)], axis=0
-        )
-        high, low_part = split(flat)
-        out = jnp.dot(high, pairing, preferred_element_type=jnp.float32)
-        out = out + jnp.dot(low_part, pairing, preferred_element_type=jnp.float32)
-        out = jnp.concatenate(
-            [out[k * pairs : (k + 1) * pairs] for k in range(width // slab)], axis=1
-        )
-        half = width // 2
-        pooled_ref[:, pl.ds(pl.multiple_of(column * half, 128), half)] = out
-
-    place(three_ref[me], me)
-    for i in range(1, owners):
-        copies[owners - i - 1].wait_recv()
-        place(landed[i], lax.rem(me + i, owners))
-    for c in copies:
-        c.wait_send()
+    pairing = jnp.where(i >> 1 == o, 0.25, 0.0).astype(jnp.bfloat16)
+    pieces = [landed[lax.rem(c - me + owners, owners)] for c in range(owners)]
+    x = jnp.concatenate(pieces, axis=1)
+    rows_ref[...] = x
+    sums = jnp.concatenate(
+        [x[2 * p : 2 * p + 1] + x[2 * p + 1 : 2 * p + 2] for p in range(pairs)], axis=0
+    )
+    count = owners * width // slab
+    flat = jnp.concatenate([sums[:, k * slab : (k + 1) * slab] for k in range(count)], axis=0)
+    high, low_part = split(flat)
+    out = jnp.dot(high, pairing, preferred_element_type=jnp.float32)
+    out = out + jnp.dot(low_part, pairing, preferred_element_type=jnp.float32)
+    pooled_ref[...] = jnp.concatenate(
+        [out[k * pairs : (k + 1) * pairs] for k in range(count)], axis=1
+    )
 
 
 def share(three):
     owners, each, width = three.shape
+    landed = pl.pallas_call(
+        functools.partial(share_kernel, owners),
+        out_shape=jax.ShapeDtypeStruct(three.shape, jnp.float32),
+        in_specs=[pl.BlockSpec(memory_space=pltpu.HBM)],
+        out_specs=pl.BlockSpec(memory_space=pltpu.HBM),
+        scratch_shapes=[
+            pltpu.SemaphoreType.DMA((owners,)),
+            pltpu.SemaphoreType.DMA((owners,)),
+            pltpu.SemaphoreType.DMA,
+        ],
+        compiler_params=pltpu.CompilerParams(collective_id=1, has_side_effects=True),
+        name="share",
+    )(three)
     return pl.pallas_call(
-        functools.partial(share_kernel, owners),
+        finish_kernel,
         out_shape=[
             jax.ShapeDtypeStruct((each, owners * width), jnp.float32),
             jax.ShapeDtypeStruct((each // 2, owners * width // 2), jnp.float32),
         ],
         in_specs=[pl.BlockSpec(memory_space=pltpu.VMEM)],
         out_specs=[pl.BlockSpec(memory_space=pltpu.VMEM)] * 2,
-        scratch_shapes=[
-            pltpu.VMEM(three.shape, jnp.float32),
-            pltpu.SemaphoreType.DMA((owners,)),
-            pltpu.SemaphoreType.DMA((owners,)),
-        ],
-        compiler_params=pltpu.CompilerParams(collective_id=1, has_side_effects=True),
-        name="share",
-    )(three)
+        name="finish",
+    )(landed)
 
 
 def body(parts, owners, source, low_row, weight_low):

time: 95.5 us -> 88 us (0.921)
  Pallas kernels: 91.6 us -> 87.1 us
  local copies, waits for them, and re-layouts: 2.8 us -> 0 us
    unnamed x2 -> x0, local copies, waits for them, and re-layouts: 2.8 us -> none
    pallas_call x1, Pallas kernels: 11.8 us -> 9.32 us  [pyramid(): pl.pallas_call(functools.partial(pyramid_kernel, total, parts), grid=(wid...]
    pallas_call x1, Pallas kernels: 74.2 us -> 72 us  [exchange(): pl.pallas_call(functools.partial(exchange_kernel, total, parts), out_shap...]
    pallas_call x1 -> x2, Pallas kernels: 5.58 us -> 5.79 us  [the longest x1 4.17 us: share(): pl.pallas_call(functools.partial(share_kernel, owners), out_shape=jax.Sha...]
where the time goes in v3:
time: 88 us; the launch traced here: 87.7 us
  Pallas kernels  87.1 us (99%)
    pallas_call x1, Pallas kernels, exchange(): pl.pallas_call(functools.partial(exchange_kernel, total, parts), out_shap...  72 us
    pallas_call x1, Pallas kernels, pyramid(): pl.pallas_call(functools.partial(pyramid_kernel, total, parts), grid=(wid...  9.32 us
    pallas_call x1, Pallas kernels, share(): pl.pallas_call(functools.partial(share_kernel, owners), out_shape=jax.Sha...  4.17 us

profile of v3, /device:TPU:0, one launch (start us, length us, event | category | flops | bytes accessed | tf_op | source)
XLA Modules:
  0.0 87.7 jit_solution(14758116493581582067)
XLA Ops:
  0.6 72.0 %halo.1.recv_ref = f32[144,8192]{1,0:T(8,128)} custom-call(f32[128,8192]{1,0:T(8,128)} %own_ref.1), custom_call_target="tpu_custom_call" | custom-call | tf_op jit(solution)/shard_map/halo/pallas_call | solution.py:227
  72.6 9.3 %pyramid.1 = (f32[128,8192]{1,0:T(8,128)}, f32[64,4096]{1,0:T(8,128)}, f32[32,2048]{1,0:T(8,128)}, f32[4,4,1024]{2,1,0:T(4,128)}) custom-call(s32[8,128]{1,0:T(8,128)} %bitcast.2, f32[8,128]{1,0:T(8,128)} %bitcast.3, f32[128,8192]{1,0:T(8,128)} %own_ref.1, f32[144,8192]{1,0:T(8,128)} %halo.1.recv_ref), custom_call_target="tpu_custom_call" | custom-call | tf_op jit(solution)/shard_map/pyramid/pallas_call | solution.py:322
  81.9 4.2 %share.1.landed = f32[4,4,1024]{2,1,0:T(4,128)} custom-call(f32[4,4,1024]{2,1,0:T(4,128)} %get-tuple-element.14.three_ref), custom_call_target="tpu_custom_call" | custom-call | tf_op jit(solution)/shard_map/share/pallas_call | solution.py:396
  86.1 1.6 %finish.1 = (f32[4,4096]{1,0:T(4,128)}, f32[2,2048]{1,0:T(2,128)}) custom-call(f32[4,4,1024]{2,1,0:T(4,128)} %share.1.landed), custom_call_target="tpu_custom_call" | custom-call | tf_op jit(solution)/shard_map/finish/pallas_call | solution.py:409
